TPU v7x, 256 devices: a whole 4x4x8 slice. The times are simulated.
256 devices in a mesh: gx: 4 (over z_lo), gy: 8 (over x, z_hi), gz: 8 (over y, core).
Axes of the slice: x: 4, y: 4, z: 8 (z_hi: 2, z_lo: 4; z = z_hi * 4 + z_lo), core: 2. Of those that a mesh axis runs over, the one named last changes fastest.
Arguments:
- attn_out: bfloat16 [16384, 8192], P('gx', ('gy', 'gz')), may hold values from -16 to 16
- out_grad: bfloat16 [16384, 8192], P('gx', ('gz', 'gy')), may hold values from -0.046875 to 0.046875
- valid_counts: int32 [16], P('gx'), may hold values from 128 to 1024
Outputs:
- weight_grad: float32 [8192, 8192], P(('gy', 'gx'), 'gz')
Inputs may be any that keep to these rules, and one draw needn't show every extreme that they name: `valid_counts`: valid tokens of a packed row come first, padding after.
All inputs are finite; a program needn't handle non-finite values.
Results may differ from a plain program's by a relative error of at most 0.0003.
Values may be sent and summed in bfloat16 or wider, within the bound.
A program may use at most 64 MiB of HBM per device.

v0:
```python
import jax
import jax.numpy as jnp
from jax import lax
from jax.sharding import Mesh
from jax.sharding import PartitionSpec as P

GY = ("gy_0", "gy_1")
GY_GZ = ("gy_0", "gy_1", "gz")
GZ_GY = ("gz", "gy_0", "gy_1")
GY_GX = ("gy_0", "gy_1", "gx")


def whole_of(value, axes, dim):
    out = value
    for number in range(len(axes) - 1, -1, -1):
        out = lax.all_gather(out, axes[number], axis=dim, tiled=True)
    return out


def split_up(value, dim, peers):
    lengths = value.shape
    tiles = value.reshape(*lengths[:dim], peers, lengths[dim] // peers, *lengths[dim + 1 :])
    return jnp.moveaxis(tiles, dim, 0)


def summed_on_arrival(value, axis, dim):
    tiles = split_up(value, dim, lax.axis_size(axis))
    arrived = lax.all_to_all(tiles, axis, split_axis=0, concat_axis=0, tiled=True)
    return arrived.sum(axis=0)


def transpose_product(inputs, grads):
    return lax.dot_general(
        inputs, grads, (((0,), (0,)), ((), ())), preferred_element_type=jnp.float32
    )


def shards(attn_out, out_grad, valid_counts):
    rows_here = valid_counts.shape[0]
    slot_count = attn_out.shape[0] // rows_here
    positions = lax.broadcasted_iota(jnp.int32, (rows_here, slot_count), 1)
    kept_rows = (positions < valid_counts[:, None]).reshape(-1)
    gathered_inputs = lax.all_gather(attn_out, "gz", axis=1, tiled=True)
    gathered_grads = whole_of(out_grad, GY, 1)
    masked = jnp.where(kept_rows[:, None], gathered_grads, jnp.zeros((), gathered_grads.dtype))
    partial_grad = transpose_product(gathered_inputs, masked)
    return summed_on_arrival(partial_grad, "gx", 0)


def solution(mesh):
    split = Mesh(
        mesh.devices.reshape(mesh.shape["gx"], 4, 2, mesh.shape["gz"]), ("gx", "gy_0", "gy_1", "gz")
    )
    return jax.shard_map(
        shards,
        mesh=split,
        in_specs=(P("gx", GY_GZ), P("gx", GZ_GY), P("gx")),
        out_specs=P(GY_GX, "gz"),
        check_vma=False,
    )
```

profile of v0, /device:TPU:8, one launch (start us, length us, event | category | flops | bytes accessed | tf_op | source)
XLA Modules:
  0.0 345.3 jit_solution(17290514149555261762)
XLA Ops:
  6.5 0.0 all-gather.4.cloned.1.call-start
  6.5 0.7 all-gather.4.cloned.1.call-update
  7.3 0.0 all-gather.8.cloned.1.call-start
  7.3 0.7 all-gather.8.cloned.1.call-update
  8.0 0.0 all-gather.6.cloned.1.call-start
  8.1 69.1 %all-gather.4.cloned.1.call-done = bf16[4096,256]{1,0:T(8,128)(2,1)} async-done(((bf16[4096,128]{1,0:T(8,128)(2,1)}), bf16[4096,256]{1,0:T(8,128)(2,1)}) %all-gather.4.cloned.1.call-update) | async-done | bytes 2097168 | tf_op jit(solution)/shard_map/all_gather | solution.py:16
  77.1 0.0 all-gather.6.cloned.1.call-update
  77.2 0.7 fusion.4
  77.9 53.2 %all-gather.8.cloned.1.call-done = bf16[4096,1024]{1,0:T(8,128)(2,1)} async-done(((bf16[4096,128]{1,0:T(8,128)(2,1)}), bf16[4096,1024]{1,0:T(8,128)(2,1)}) %all-gather.8.cloned.1.call-update) | async-done | bytes 8388624 | tf_op jit(solution)/shard_map/all_gather | solution.py:43
  131.1 92.2 %all-gather.6.cloned.1.call-done = bf16[4096,1024]{1,0:T(8,128)(2,1)} async-done(((bf16[4096,256]{1,0:T(8,128)(2,1)}), bf16[4096,1024]{1,0:T(8,128)(2,1)}) %all-gather.6.cloned.1.call-update) | async-done | bytes 8388624 | tf_op jit(solution)/shard_map/all_gather | solution.py:16
  223.3 15.3 %fusion = f32[1024,1024]{0,1:T(8,128)S(1)} fusion(bf16[4096,1024]{1,0:T(8,128)(2,1)} %all-gather.8.cloned.1.call-done, bf16[4096,1024]{1,0:T(8,128)(2,1)} %all-gather.6.cloned.1.call-done, pred[4096]{0:T(1024)(128)(4,1)S(1)} %bitcast.10), kind=kOutput, calls=%fused_computation | convolution fusion | flops 8594128896 | bytes 20975616 | tf_op jit(solution)/shard_map/dot_general | solution.py:33
  238.6 96.5 %all_to_all.5 = f32[4,256,1024]{2,1,0:T(8,128)} all-to-all(f32[4,256,1024]{2,1,0:T(8,128)S(1)} %bitcast.9), channel_id=1, replica_groups=mesh['gx'=4,'gy_0'=4,'gy_1'=2,'gz'=8] {'gx'}, dimensions={0} | all-to-all | bytes 8388608 | tf_op jit(solution)/shard_map/all_to_all | solution.py:28
  335.1 3.7 %reduce_sum.9 = f32[256,1024]{1,0:T(8,128)} reduce(f32[4,256,1024]{2,1,0:T(8,128)} %all_to_all.5, f32[]{:T(128)} %constant.1.clone.1), dimensions={0}, to_apply=%region_0.1 | reduce | flops 786432 | bytes 5242884 | tf_op jit(solution)/shard_map/reduce_sum | solution.py:29
  (1 shorter events, 0.0 us)
Async XLA Ops:
  6.5 70.6 %all-gather.4.cloned.1.call-start = ((), (), s32[]{:S(2)}) async-start(), calls=%async_computation.1 | async-start | bytes 3145728 | tf_op jit(solution)/shard_map/all_gather | solution.py:16
  7.3 123.8 %all-gather.8.cloned.1.call-start = ((), (), s32[]{:S(2)}) async-start(), calls=%async_computation.3 | async-start | bytes 9437184 | tf_op jit(solution)/shard_map/all_gather | solution.py:43
  8.0 215.3 %all-gather.6.cloned.1.call-start = ((), (), s32[]{:S(2)}) async-start(), calls=%async_computation.2 | async-start | bytes 10485760 | tf_op jit(solution)/shard_map/all_gather | solution.py:16
Sparse Core Ops, SparseCore 0:
  9.1 67.9 all-gather.3
  79.0 52.0 all-gather.7
  132.9 90.3 all-gather.5
where the time goes:
time: 345 us
  waiting for transfers between devices  216 us (63%)
  blocking collectives  96.5 us (28%)
  matrix products  15.3 us (4%)
  between operations  13.1 us (4%)
  other arithmetic  4.42 us (1%)
    all_gather x2, waiting for transfers between devices, whole_of(): out = lax.all_gather(out, axes[number], axis=dim, tiled=True)  161 us
    all_to_all x1, blocking collectives, summed_on_arrival(): lax.all_to_all(tiles, axis, split_axis=0, concat_axis=0, tiled=True)  96.5 us
    all_gather x1, waiting for transfers between devices, shards(): gathered_inputs = lax.all_gather(attn_out, 'gz', axis=1, tiled=True)  53.2 us
    dot_general x1, matrix products, transpose_product(): lax.dot_general(inputs, grads, (((0,), (0,)), ((), ())), preferred_elemen...  15.3 us
  transfers between devices with their start and end apart: 3, of which 3 were waited for; matrix products, arithmetic and copies ran while one was open for 0% of the time, Pallas kernels for 0%

commit v1 on v0

--- a/solution.py
+++ b/solution.py
@@ -8,6 +8,17 @@
 GY_GZ = ("gy_0", "gy_1", "gz")
 GZ_GY = ("gz", "gy_0", "gy_1")
 GY_GX = ("gy_0", "gy_1", "gx")
+
+
+def gather_around(value, axis, dim):
+    ways = lax.axis_size(axis)
+    pieces = [value]
+    for far in range(1, ways):
+        pieces.append(
+            lax.ppermute(pieces[far - 1], axis, [(d, (d - 1) % ways) for d in range(ways)])
+        )
+    line = jnp.concatenate(pieces, axis=dim)
+    return jnp.roll(line, lax.axis_index(axis) * value.shape[dim], axis=dim)
 
 
 def whole_of(value, axes, dim):
@@ -40,7 +51,7 @@
     slot_count = attn_out.shape[0] // rows_here
     positions = lax.broadcasted_iota(jnp.int32, (rows_here, slot_count), 1)
     kept_rows = (positions < valid_counts[:, None]).reshape(-1)
-    gathered_inputs = lax.all_gather(attn_out, "gz", axis=1, tiled=True)
+    gathered_inputs = gather_around(attn_out, "gz", 1)
     gathered_grads = whole_of(out_grad, GY, 1)
     masked = jnp.where(kept_rows[:, None], gathered_grads, jnp.zeros((), gathered_grads.dtype))
     partial_grad = transpose_product(gathered_inputs, masked)

time: 345 us -> 316 us (0.916)
  waiting for transfers between devices: 216 us -> 144 us
  local copies, waits for them, and re-layouts: 0.01 us -> 26.4 us
  starting transfers between devices: 0.08 us -> 12.8 us
    all_gather x2, waiting for transfers between devices: 161 us -> 69.8 us  [whole_of(): out = lax.all_gather(out, axes[number], axis=dim, tiled=True)]
    ppermute x0 -> x7, waiting for transfers between devices: none -> 73.5 us  [gather_around(): lax.ppermute(pieces[far - 1], axis, [(d, (d - 1) % ways) for d in range(w...]
    all_gather x1 -> x0, waiting for transfers between devices: 53.2 us -> none  [shards(): gathered_inputs = lax.all_gather(attn_out, 'gz', axis=1, tiled=True)]
    unnamed x1 -> x22, local copies, waits for them, and re-layouts: 0.01 us -> 25.3 us
    ppermute x0 -> x7, starting transfers between devices: none -> 12.7 us  [gather_around(): lax.ppermute(pieces[far - 1], axis, [(d, (d - 1) % ways) for d in range(w...]
  transfers between devices with their start and end apart: 3 -> 9, of which waited for: 3 -> 8; matrix products, arithmetic and copies ran while one was open for 0% -> 8% of each run, Pallas kernels for 0% -> 0%
where the time goes in v1:
time: 316 us; the launch traced here: 314 us
  waiting for transfers between devices  144 us (46%)
  blocking collectives  97.2 us (31%)
  local copies, waits for them, and re-layouts  26.4 us (8%)
  matrix products  15.3 us (5%)
  between operations  13.4 us (4%)
  starting transfers between devices  12.8 us (4%)
  other arithmetic  4.42 us (1%)
    all_to_all x1, blocking collectives, summed_on_arrival(): lax.all_to_all(tiles, axis, split_axis=0, concat_axis=0, tiled=True)  97.2 us
    ppermute x7, waiting for transfers between devices, gather_around(): lax.ppermute(pieces[far - 1], axis, [(d, (d - 1) % ways) for d in range(w...  73.5 us
    all_gather x2, waiting for transfers between devices, whole_of(): out = lax.all_gather(out, axes[number], axis=dim, tiled=True)  69.8 us
    unnamed x22, local copies, waits for them, and re-layouts  25.3 us
    dot_general x1, matrix products, transpose_product(): lax.dot_general(inputs, grads, (((0,), (0,)), ((), ())), preferred_elemen...  15.3 us
    ppermute x7, starting transfers between devices, gather_around(): lax.ppermute(pieces[far - 1], axis, [(d, (d - 1) % ways) for d in range(w...  12.7 us
  transfers between devices with their start and end apart: 9, of which 8 were waited for; matrix products, arithmetic and copies ran while one was open for 8% of the time, Pallas kernels for 0%

profile of v1, /device:TPU:8, one launch (start us, length us, event | category | flops | bytes accessed | tf_op | source)
XLA Modules:
  0.0 313.6 jit_solution(11945423491475501619)
XLA Ops:
  7.3 69.8 %all-gather.3.cloned.1.call-done = bf16[4096,256]{1,0:T(8,128)(2,1)} async-done(((bf16[4096,128]{1,0:T(8,128)(2,1)}), bf16[4096,256]{1,0:T(8,128)(2,1)}) %all-gather.3.cloned.1.call-update) | async-done | bytes 2097168 | tf_op jit(solution)/shard_map/all_gather | solution.py:27
  77.2 12.6 %collective-permute-done = bf16[4096,128]{1,0:T(8,128)(2,1)S(1)} collective-permute-done((bf16[4096,128]{1,0:T(8,128)(2,1)}, bf16[4096,128]{1,0:T(8,128)(2,1)S(1)}, u32[]{:S(2)}, u32[]{:S(2)}) %collective-permute-start) | collective-permute-done | bytes 1048608 | tf_op jit(solution)/shard_map/ppermute | solution.py:18
  89.8 1.8 collective-permute-start.1
  91.6 12.3 %collective-permute-done.1 = bf16[4096,128]{1,0:T(8,128)(2,1)S(1)} collective-permute-done((bf16[4096,128]{1,0:T(8,128)(2,1)S(1)}, bf16[4096,128]{1,0:T(8,128)(2,1)S(1)}, u32[]{:S(2)}, u32[]{:S(2)}) %collective-permute-start.1) | collective-permute-done | bytes 1048608 | tf_op jit(solution)/shard_map/ppermute | solution.py:18
  103.9 2.3 collective-permute-start.2
  106.3 12.3 %collective-permute-done.2 = bf16[4096,128]{1,0:T(8,128)(2,1)S(1)} collective-permute-done((bf16[4096,128]{1,0:T(8,128)(2,1)S(1)}, bf16[4096,128]{1,0:T(8,128)(2,1)S(1)}, u32[]{:S(2)}, u32[]{:S(2)}) %collective-permute-start.2) | collective-permute-done | bytes 1048608 | tf_op jit(solution)/shard_map/ppermute | solution.py:18
  119.5 2.3 collective-permute-start.3
  121.9 12.3 %collective-permute-done.3 = bf16[4096,128]{1,0:T(8,128)(2,1)} collective-permute-done((bf16[4096,128]{1,0:T(8,128)(2,1)S(1)}, bf16[4096,128]{1,0:T(8,128)(2,1)}, u32[]{:S(2)}, u32[]{:S(2)}) %collective-permute-start.3) | collective-permute-done | bytes 1048608 | tf_op jit(solution)/shard_map/ppermute | solution.py:18
  134.2 2.3 collective-permute-start.4
  137.2 2.4 constant_dynamic-update-slice_fusion.15
  139.7 9.4 %collective-permute-done.4 = bf16[4096,128]{1,0:T(8,128)(2,1)} collective-permute-done((bf16[4096,128]{1,0:T(8,128)(2,1)}, bf16[4096,128]{1,0:T(8,128)(2,1)}, u32[]{:S(2)}, u32[]{:S(2)}) %collective-permute-start.4) | collective-permute-done | bytes 1048608 | tf_op jit(solution)/shard_map/ppermute | solution.py:18
  149.1 2.2 collective-permute-start.5
  152.5 1.2 constant_dynamic-update-slice_fusion.13
  153.6 2.3 constant_dynamic-update-slice_fusion.12
  155.9 8.0 %collective-permute-done.5 = bf16[4096,128]{1,0:T(8,128)(2,1)S(1)} collective-permute-done((bf16[4096,128]{1,0:T(8,128)(2,1)}, bf16[4096,128]{1,0:T(8,128)(2,1)S(1)}, u32[]{:S(2)}, u32[]{:S(2)}) %collective-permute-start.5) | collective-permute-done | bytes 1048608 | tf_op jit(solution)/shard_map/ppermute | solution.py:18
  163.9 1.8 collective-permute-start.6
  165.7 2.4 constant_dynamic-update-slice_fusion.11
  168.1 2.3 constant_dynamic-update-slice_fusion.10
  171.6 6.5 %collective-permute-done.6 = bf16[4096,128]{1,0:T(8,128)(2,1)S(1)} collective-permute-done((bf16[4096,128]{1,0:T(8,128)(2,1)S(1)}, bf16[4096,128]{1,0:T(8,128)(2,1)S(1)}, u32[]{:S(2)}, u32[]{:S(2)}) %collective-permute-start.6) | collective-permute-done | bytes 1048608 | tf_op jit(solution)/shard_map/ppermute | solution.py:18
  183.7 2.4 constant_dynamic-update-slice_fusion.3
  186.0 2.3 constant_dynamic-update-slice_fusion.2
  190.6 15.3 %fusion = f32[1024,1024]{1,0:T(8,128)S(1)} fusion(bf16[4096,1024]{1,0:T(8,128)(2,1)} %all-gather.5.cloned.1.call-done, bf16[4096,2048]{1,0:T(8,128)(2,1)} %constant_dynamic-update-slice_fusion, s32[]{:T(128)S(6)} %select_n.18, pred[4096]{0:T(1024)(128)(4,1)S(1)} %bitcast.7), kind=kOutput, calls=%fused_computation | convolution fusion | flops 8594128896 | bytes 20975620 | tf_op jit(solution)/shard_map/dot_general | solution.py:44
  205.9 97.2 %all_to_all.5 = f32[4,256,1024]{2,1,0:T(8,128)} all-to-all(f32[4,256,1024]{2,1,0:T(8,128)S(1)} %bitcast.6), channel_id=1, replica_groups=mesh['gx'=4,'gy_0'=4,'gy_1'=2,'gz'=8] {'gx'}, dimensions={0} | all-to-all | bytes 8388608 | tf_op jit(solution)/shard_map/all_to_all | solution.py:39
  303.1 3.7 %reduce_sum.9 = f32[256,1024]{1,0:T(8,128)} reduce(f32[4,256,1024]{2,1,0:T(8,128)} %all_to_all.5, f32[]{:T(128)} %constant.31.clone.1), dimensions={0}, to_apply=%region_0.1 | reduce | flops 786432 | bytes 5242884 | tf_op jit(solution)/shard_map/reduce_sum | solution.py:40
  (23 shorter events, 12.6 us)
Async XLA Ops:
  6.5 172.6 %copy-start = (bf16[4096,128]{1,0:T(8,128)(2,1)S(1)}, bf16[4096,128]{1,0:T(8,128)(2,1)}, u32[]{:S(2)}) copy-start(bf16[4096,128]{1,0:T(8,128)(2,1)} %param.3) | copy-start | bytes 3145732
  6.5 70.6 %all-gather.3.cloned.1.call-start = ((), (), s32[]{:S(2)}) async-start(), calls=%async_computation.1 | async-start | bytes 3145728 | tf_op jit(solution)/shard_map/all_gather | solution.py:27
  7.3 183.3 %all-gather.5.cloned.1.call-start = ((), (), s32[]{:S(2)}) async-start(), calls=%async_computation.2 | async-start | bytes 10485760 | tf_op jit(solution)/shard_map/all_gather | solution.py:27
  77.2 12.7 %collective-permute-start = (bf16[4096,128]{1,0:T(8,128)(2,1)}, bf16[4096,128]{1,0:T(8,128)(2,1)S(1)}, u32[]{:S(2)}, u32[]{:S(2)}) collective-permute-start(bf16[4096,128]{1,0:T(8,128)(2,1)} %param.3), channel_id=1, source_target_pairs={{0,7},{1,0},{2,1},{3,2},{4,3},{5,4},{6,5},{7,6},{8,15},{9,8},{10,9... | collective-permute-start | bytes 3145736 | tf_op jit(solution)/shard_map/ppermute | solution.py:18
  89.8 14.1 %collective-permute-start.1 = (bf16[4096,128]{1,0:T(8,128)(2,1)S(1)}, bf16[4096,128]{1,0:T(8,128)(2,1)S(1)}, u32[]{:S(2)}, u32[]{:S(2)}) collective-permute-start(bf16[4096,128]{1,0:T(8,128)(2,1)S(1)} %collective-permute-done), channel_id=1, source_target_pairs={{0,7},{1,0},{2,1},{3,2},{4,3},{5,4},{6,5},{7,6},{8,15},{9,8},{10,9... | collective-permute-start | bytes 3145736 | tf_op jit(solution)/shard_map/ppermute | solution.py:18
  103.9 14.6 %collective-permute-start.2 = (bf16[4096,128]{1,0:T(8,128)(2,1)S(1)}, bf16[4096,128]{1,0:T(8,128)(2,1)S(1)}, u32[]{:S(2)}, u32[]{:S(2)}) collective-permute-start(bf16[4096,128]{1,0:T(8,128)(2,1)S(1)} %collective-permute-done.1), channel_id=1, source_target_pairs={{0,7},{1,0},{2,1},{3,2},{4,3},{5,4},{6,5},{7,6},{8,15},{9,8},{10,9... | collective-permute-start | bytes 3145736 | tf_op jit(solution)/shard_map/ppermute | solution.py:18
  118.6 1.0 copy-start.1
  119.5 14.6 %collective-permute-start.3 = (bf16[4096,128]{1,0:T(8,128)(2,1)S(1)}, bf16[4096,128]{1,0:T(8,128)(2,1)}, u32[]{:S(2)}, u32[]{:S(2)}) collective-permute-start(bf16[4096,128]{1,0:T(8,128)(2,1)S(1)} %collective-permute-done.2), channel_id=1, source_target_pairs={{0,7},{1,0},{2,1},{3,2},{4,3},{5,4},{6,5},{7,6},{8,15},{9,8},{10,9... | collective-permute-start | bytes 3145736 | tf_op jit(solution)/shard_map/ppermute | solution.py:18
  134.2 14.9 %collective-permute-start.4 = (bf16[4096,128]{1,0:T(8,128)(2,1)}, bf16[4096,128]{1,0:T(8,128)(2,1)}, u32[]{:S(2)}, u32[]{:S(2)}) collective-permute-start(bf16[4096,128]{1,0:T(8,128)(2,1)} %collective-permute-done.3), channel_id=1, source_target_pairs={{0,7},{1,0},{2,1},{3,2},{4,3},{5,4},{6,5},{7,6},{8,15},{9,8},{10,9... | collective-permute-start | bytes 3145736 | tf_op jit(solution)/shard_map/ppermute | solution.py:18
  137.2 45.4 %copy-start.2 = (bf16[4096,128]{1,0:T(8,128)(2,1)S(1)}, bf16[4096,128]{1,0:T(8,128)(2,1)}, u32[]{:S(2)}) copy-start(bf16[4096,128]{1,0:T(8,128)(2,1)} %copy-done.1) | copy-start | bytes 3145732
  149.1 14.8 %collective-permute-start.5 = (bf16[4096,128]{1,0:T(8,128)(2,1)}, bf16[4096,128]{1,0:T(8,128)(2,1)S(1)}, u32[]{:S(2)}, u32[]{:S(2)}) collective-permute-start(bf16[4096,128]{1,0:T(8,128)(2,1)} %collective-permute-done.4), channel_id=1, source_target_pairs={{0,7},{1,0},{2,1},{3,2},{4,3},{5,4},{6,5},{7,6},{8,15},{9,8},{10,9... | collective-permute-start | bytes 3145736 | tf_op jit(solution)/shard_map/ppermute | solution.py:18
  163.9 14.1 %collective-permute-start.6 = (bf16[4096,128]{1,0:T(8,128)(2,1)S(1)}, bf16[4096,128]{1,0:T(8,128)(2,1)S(1)}, u32[]{:S(2)}, u32[]{:S(2)}) collective-permute-start(bf16[4096,128]{1,0:T(8,128)(2,1)S(1)} %collective-permute-done.5), channel_id=1, source_target_pairs={{0,7},{1,0},{2,1},{3,2},{4,3},{5,4},{6,5},{7,6},{8,15},{9,8},{10,9... | collective-permute-start | bytes 3145736 | tf_op jit(solution)/shard_map/ppermute | solution.py:18
Sparse Core Ops, SparseCore 0:
  9.1 67.9 all-gather.2
  78.9 85.4 all-gather.4
